TPU v7x, 32 devices: a whole 2x2x4 slice. The times are simulated.
32 devices in a mesh: seq: 16 (over z, y, core), dp: 2 (over x).
Axes of the slice: x: 2, y: 2, z: 4, core: 2. Of those that a mesh axis runs over, the one named last changes fastest.
Arguments:
- acceptors: bfloat16 [2, 2048, 2560], P('dp', 'seq'), may hold values from -2 to 2
- lookups: bfloat16 [2, 2048, 2560], P('dp', 'seq'), may hold values from -0.625 to 0.625
- payloads: bfloat16 [2, 2048, 2560], P('dp', 'seq'), may hold values from -6 to 6
- lagged_fading_source: bfloat16 [2, 2048, 2560], P('dp', 'seq'), may hold values from -6 to 6
- response_cotangent: bfloat16 [2, 2048, 2560], P('dp', 'seq'), may hold values from -5 to 5
- fading_lowering_array: bfloat16 [2560, 128], replicated, may hold values from -0.125 to 0.125
- fading_raising_array: bfloat16 [2560, 128], replicated, may hold values from -1.25 to 1.25
- feature_fading_speed: float32 [2560], replicated, may hold values from 2.3251488e-05 to 0.125
- present_reward: float32 [2560], replicated, may hold values from 1.4142135 to 11.313708
Outputs:
- mixed: bfloat16 [2, 2048, 2560], P('dp', 'seq')
- grad_receptance: bfloat16 [2, 2048, 2560], P('dp', 'seq')
- lookup_deriv: bfloat16 [2, 2048, 2560], P('dp', 'seq')
- payload_deriv: bfloat16 [2, 2048, 2560], P('dp', 'seq')
- grad_decay_input: bfloat16 [2, 2048, 2560], P('dp', 'seq')
- grad_lora_a: float32 [2560, 128], P('dp')
- grad_lora_b: float32 [2560, 128], P('dp')
- grad_time_decay: float32 [2560], P('dp')
- present_reward_deriv: float32 [2560], P('dp')
All inputs are finite; a program needn't handle non-finite values.
Results may differ from a plain program's by a relative error of at most 0.006.
Values sent between devices are 32-bit elements.
A program may use at most 320 MiB of HBM per device.

v0:
```python
import jax
import jax.numpy as jnp
from jax import lax
from jax.sharding import PartitionSpec as P

ATTENDER_TOTAL = 40
LANE_TOTAL = 64
BLOCK = 64
HIGH = lax.Precision.HIGHEST


def carried_in(part, axis, combine, identity, reverse):
    count = lax.axis_size(axis)
    place = lax.axis_index(axis)
    ahead = count - 1 - place if reverse else place
    gathered = jax.tree.map(lambda a: lax.all_gather(a, axis), part)
    state = jax.tree.map(lambda a, e: jnp.zeros_like(a) + jnp.asarray(e, a.dtype), part, identity)

    def one(hop, state):
        source = count - 1 - hop if reverse else hop
        return combine(
            state, jax.tree.map(lambda a: lax.dynamic_index_in_dim(a, source, 0, False), gathered)
        )

    return lax.fori_loop(0, ahead, one, state)


def contract(pattern, left, right):
    return jnp.einsum(pattern, left, right, precision=HIGH, preferred_element_type=jnp.float32)


def decay_log_values(input_rows, fading_lowering_array, fading_raising_array, feature_fading_speed):
    apply_projection = jnp.dot(
        input_rows, fading_lowering_array, preferred_element_type=jnp.float32
    )
    smoothed_values = jnp.tanh(apply_projection)
    gate_portion = smoothed_values.astype(jnp.bfloat16)
    rank_projection = lax.dot_general(
        gate_portion,
        fading_raising_array,
        (((1,), (1,)), ((), ())),
        preferred_element_type=jnp.float32,
    )
    return (
        smoothed_values,
        gate_portion,
        -feature_fading_speed[None, :] * jnp.exp(rank_projection),
    )


def compose(decays, own_states, backward):

    def advance(carry, member):
        run_decay, run_state = carry
        decay, own_state = member
        return ((run_decay * decay, decay[..., None] * run_state + own_state), carry)

    initial = (
        jnp.ones(decays.shape[1:], jnp.float32),
        jnp.zeros(own_states.shape[1:], jnp.float32),
    )
    return lax.scan(advance, initial, (decays, own_states), reverse=backward)


def follow(earlier, later):
    return (earlier[0] * later[0], later[0][..., None] * earlier[1] + later[1])


def temporal_blend_sublevel(
    acceptor_lines,
    lookups,
    payloads,
    incoming_cotangent,
    fading_exponent,
    reward_by_attender,
    adjacent_shardlink,
):
    inclusive = jnp.cumsum(fading_exponent, axis=1)
    exclusive = inclusive - fading_exponent
    middle = inclusive[:, BLOCK // 2 - 1 : BLOCK // 2]
    overall = inclusive[:, -1]
    entering = jnp.exp(exclusive)
    leaving = jnp.exp(overall[:, None] - inclusive)
    upward = jnp.exp(exclusive - middle)
    downward = jnp.exp(middle - inclusive)
    decays = jnp.exp(overall)
    reached = acceptor_lines * entering
    faded_keys = lookups * leaving
    own_states = contract("nchk,nchv->nhkv", faded_keys, payloads)
    pull_states = contract("nchk,nchv->nhkv", reached, incoming_cotangent)
    starts, block_ends = adjacent_shardlink(decays, own_states, pull_states)
    position = jnp.arange(BLOCK)
    beneath = position[:, None] > position[None, :]
    early_recept = acceptor_lines * upward
    late_keys = lookups * downward
    scores = jnp.where(beneath, contract("nthk,nshk->nhts", early_recept, late_keys), 0.0)
    present_contribution = jnp.sum(acceptor_lines * reward_by_attender * lookups, axis=-1)[
        ..., None
    ]
    blended_response = (
        contract("nhts,nshv->nthv", scores, payloads)
        + present_contribution * payloads
        + contract("nthk,nhkv->nthv", reached, starts)
    )
    grad_start = decays[..., None] * block_ends + pull_states
    products = jnp.where(beneath, contract("nthv,nshv->nhts", incoming_cotangent, payloads), 0.0)
    agreement_verify = jnp.sum(payloads * incoming_cotangent, axis=-1)[..., None]
    memory_acceptors = entering * contract(
        "nhkv,nthv->nthk", starts, incoming_cotangent
    ) + upward * contract("nhts,nshk->nthk", products, late_keys)
    memory_lookup_lines = leaving * contract(
        "nhkv,nthv->nthk", block_ends, payloads
    ) + downward * contract("nhst,nshk->nthk", products, early_recept)
    payload_deriv = (
        contract("nthk,nhkv->nthv", faded_keys, block_ends)
        + contract("nhst,nshv->nthv", scores, incoming_cotangent)
        + present_contribution * incoming_cotangent
    )
    acceptor_deriv = memory_acceptors + reward_by_attender * lookups * agreement_verify
    lookup_deriv = memory_lookup_lines + reward_by_attender * acceptor_lines * agreement_verify
    present_reward_deriv = jnp.sum(acceptor_lines * lookups * agreement_verify, axis=(0, 1))
    coupling = jnp.sum(grad_start * starts, axis=-1)
    change = lookups * memory_lookup_lines - acceptor_lines * memory_acceptors
    fading_deriv = (
        coupling[:, None] + jnp.cumsum(change, axis=1) - change - acceptor_lines * memory_acceptors
    )
    return (
        blended_response,
        acceptor_deriv,
        lookup_deriv,
        payload_deriv,
        fading_deriv,
        present_reward_deriv,
    )


def sublevel_evaluation(
    reshaped_acceptors,
    reshaped_lookups,
    reshaped_payloads,
    reshaped_source,
    incoming_cotangent_reshaped,
    fading_lowering_array,
    fading_raising_array,
    feature_fading_speed,
    present_reward,
    adjacent_shardlink,
):
    smoothed_values, gate_portion, fading_exponent = decay_log_values(
        reshaped_source, fading_lowering_array, fading_raising_array, feature_fading_speed
    )
    tokens, feature_span = reshaped_acceptors.shape
    tiling_arrangement = (tokens // BLOCK, BLOCK, ATTENDER_TOTAL, LANE_TOTAL)
    collected_outcomes = temporal_blend_sublevel(
        reshaped_acceptors.astype(jnp.float32).reshape(tiling_arrangement),
        reshaped_lookups.astype(jnp.float32).reshape(tiling_arrangement),
        reshaped_payloads.astype(jnp.float32).reshape(tiling_arrangement),
        incoming_cotangent_reshaped.astype(jnp.float32).reshape(tiling_arrangement),
        fading_exponent.reshape(tiling_arrangement),
        present_reward.reshape(ATTENDER_TOTAL, LANE_TOTAL),
        adjacent_shardlink,
    )
    (
        blended_response,
        acceptor_deriv,
        lookup_deriv,
        payload_deriv,
        fading_deriv,
        present_reward_deriv,
    ) = collected_outcomes
    slope = fading_deriv.reshape(tokens, feature_span) * fading_exponent
    slope_portion = slope.astype(jnp.bfloat16)
    gate_gradient = jnp.dot(slope_portion, fading_raising_array, preferred_element_type=jnp.float32)
    projection_gradient = (gate_gradient * (1.0 - smoothed_values * smoothed_values)).astype(
        jnp.bfloat16
    )
    input_gradient = lax.dot_general(
        projection_gradient,
        fading_lowering_array,
        (((1,), (1,)), ((), ())),
        preferred_element_type=jnp.float32,
    ).astype(jnp.bfloat16)
    lowering_array_deriv = lax.dot_general(
        reshaped_source,
        projection_gradient,
        (((0,), (0,)), ((), ())),
        preferred_element_type=jnp.float32,
    )
    raising_array_deriv = lax.dot_general(
        slope_portion, gate_portion, (((0,), (0,)), ((), ())), preferred_element_type=jnp.float32
    )
    speed_deriv = jnp.sum(slope, axis=0)

    def flatten(member):
        return member.reshape(tokens, feature_span).astype(jnp.bfloat16)

    return (
        flatten(blended_response),
        flatten(acceptor_deriv),
        flatten(lookup_deriv),
        flatten(payload_deriv),
        input_gradient,
        (
            lowering_array_deriv,
            raising_array_deriv,
            speed_deriv,
            present_reward_deriv.reshape(feature_span),
        ),
    )


def shard_link(decays, own_states, pull_states):
    ahead_total, ahead = compose(decays, own_states, False)
    behind_total, behind = compose(decays, pull_states, True)
    identity = (jnp.ones_like(ahead_total[0]), jnp.zeros_like(ahead_total[1]))
    prior, state_in = carried_in(ahead_total, "seq", follow, identity, False)
    latter, grad_after = carried_in(behind_total, "seq", follow, identity, True)
    starts = ahead[0][..., None] * state_in[None] + ahead[1]
    block_ends = behind[0][..., None] * grad_after[None] + behind[1]
    return (starts, block_ends)


def per_device(
    acceptors,
    lookups,
    payloads,
    lagged_fading_source,
    response_cotangent,
    fading_lowering_array,
    fading_raising_array,
    feature_fading_speed,
    present_reward,
):
    collected_outcomes = sublevel_evaluation(
        acceptors[0],
        lookups[0],
        payloads[0],
        lagged_fading_source[0],
        response_cotangent[0],
        fading_lowering_array,
        fading_raising_array,
        feature_fading_speed,
        present_reward,
        shard_link,
    )
    sums = collected_outcomes[5]
    dp_count = lax.axis_size("dp")
    share_rows = fading_lowering_array.shape[0] // dp_count
    whole = lax.psum((sums[0], sums[1], sums[2], sums[3]), ("seq", "dp"))
    offset = lax.axis_index("dp") * share_rows
    reduced = tuple((lax.dynamic_slice_in_dim(member, offset, share_rows, 0) for member in whole))
    return (
        collected_outcomes[0][None],
        collected_outcomes[1][None],
        collected_outcomes[2][None],
        collected_outcomes[3][None],
        collected_outcomes[4][None],
        reduced[0],
        reduced[1],
        reduced[2],
        reduced[3],
    )


def solution(mesh):
    in_specs = (
        P("dp", "seq", None),
        P("dp", "seq", None),
        P("dp", "seq", None),
        P("dp", "seq", None),
        P("dp", "seq", None),
        P(),
        P(),
        P(),
        P(),
    )
    out_specs = (
        P("dp", "seq", None),
        P("dp", "seq", None),
        P("dp", "seq", None),
        P("dp", "seq", None),
        P("dp", "seq", None),
        P("dp", None),
        P("dp", None),
        P("dp"),
        P("dp"),
    )
    return jax.shard_map(
        per_device, mesh=mesh, in_specs=in_specs, out_specs=out_specs, check_vma=False
    )
```

profile of v0, /device:TPU:0, one launch (start us, length us, event | category | flops | bytes accessed | tf_op | source)
XLA Modules:
  0.0 555.1 jit_solution(3904437213683768561)
XLA Ops:
  28.6 5.5 fusion.57
  36.0 17.7 %while.66 = (s32[]{:T(128)}, f32[40,64]{1,0:T(8,128)S(1)}, f32[40,64,64]{2,1,0:T(8,128)}, f32[2,40,64]{2,1,0:T(8,128)S(1)}, f32[2,40,64,64]{2,3,1,0:T(8,128)}, /...) while((s32[]{:T(128)}, f32[40,64]{1,0:T(8,128)S(1)}, ...), condition=%wide.region_3.4_spmd.clone, body=%wide.region_2.3_spmd.clone.sunk | while | flops 499203 | bytes 6646389 | solution.py:62
  44.6 3.6 select_bitcast_fusion.4
  62.6 3.6 copy.91
  66.2 7.1 %fusion.50 = f32[2,40,64,64]{2,3,1,0:T(8,128)} fusion(f32[2,64,40,64]{1,3,2,0:T(8,128)} %copy.91, bf16[2,64,40,64]{3,2,1,0:T(8,128)(2,1)} %reshape.125, f32[2,64,40,64]{1,3,2,0:T(8,128)S(1)} %copy.89, f32[2,64,40,64]{1,3,2,0:T(8,128)} %copy.90), kind=kOutput, calls=%fused_computation.85 | convolution fusion | flops 252313600 | bytes 5898240 | tf_op jit(solution)/shard_map/nchk,nchv->nhkv/dot_general | solution.py:29
  75.7 29.7 %while.67 = (s32[]{:T(128)}, f32[40,64]{1,0:T(8,128)S(1)}, f32[40,64,64]{2,1,0:T(8,128)}, f32[2,40,64]{2,1,0:T(8,128)}, f32[2,40,64,64]{2,3,1,0:T(8,128)}, /*ind...) while((s32[]{:T(128)}, f32[40,64]{1,0:T(8,128)S(1)}, ...), condition=%wide.region_8.9_spmd.clone, body=%wide.region_7.8_spmd.clone.sunk | while | flops 499204 | bytes 9257093 | solution.py:62
  96.4 3.7 select_bitcast_fusion.5
  116.3 27.7 %all-gather = f32[640,64]{1,0:T(8,128)} all-gather(f32[40,64]{1,0:T(8,128)S(1)} %get-tuple-element.322), channel_id=2, replica_groups=mesh['seq'=16,'dp'=2] {'seq'}, dimensions={0}, use_global_device_ids=true | all-gather | bytes 174080 | tf_op jit(solution)/shard_map/all_gather | solution.py:16
  144.0 21.9 %all-gather.2 = f32[640,64]{1,0:T(8,128)} all-gather(f32[40,64]{1,0:T(8,128)S(1)} %get-tuple-element.327), channel_id=4, replica_groups=mesh['seq'=16,'dp'=2] {'seq'}, dimensions={0}, use_global_device_ids=true | all-gather | bytes 174080 | tf_op jit(solution)/shard_map/all_gather | solution.py:16
  168.8 4.1 fusion.62
  172.9 7.7 %fusion.52 = f32[2,40,64,64]{3,2,1,0:T(8,128)} fusion(f32[2,64,40,64]{1,3,2,0:T(8,128)S(1)} %copy-done.3, f32[2,64,40,64]{1,3,2,0:T(8,128)S(1)} %copy.89, f32[2,40,64]{2,1,0:T(8,128)S(1)} %get-tuple-element.494, f32[2,64,40,64]{1,3,2,0:T(8,128)S(1)} %copy-done.6, f32[2,64,40,64]{1,3,2,0:T(8,128)S(1)} %copy-done.1), kind=kOutput, calls=%fused_computation.86 | convolution fusion | flops 253296640 | bytes 6574080 | tf_op jit(solution)/shard_map/nthk,nshk->nhts/dot_general | solution.py:29
  184.8 97.0 %all-gather.9.cloned.1.call-done = f32[640,64,64]{2,1,0:T(8,128)} async-done(((f32[40,64,64]{2,1,0:T(8,128)}), f32[640,64,64]{2,1,0:T(8,128)}) %all-gather.9.cloned.1.call-update) | async-done | bytes 10485776 | tf_op jit(solution)/shard_map/all_gather | solution.py:16
  283.1 60.2 %while.65 = (s32[]{:T(128)}, f32[40,64,64]{2,1,0:T(8,128)}, s32[]{:T(128)}, f32[16,40,64]{2,1,0:T(8,128)}, f32[16,40,64,64]{3,2,1,0:T(8,128)}, /*index=5*/s32[]{:T(128)}, s32[]{:T(128)}, s32[]{:T(128)}, s32[]{:T(128)}) while((s32[]{:T(128)}, f32[40,64,64]{2,1,0:T(8,128)}, s32[]{:T(128)}, f32[16,40,64]{2,1,0:T(8,128)}, ...), condition=%wide.region_10.11_spmd, body=%wide.region_9.10_spmd.sunk | while | flops 327686 | bytes 1996947 | solution.py:25
  346.1 6.4 %fusion.24 = f32[2,40,64,64]{3,2,1,0:T(8,128)} fusion(f32[2,40,64,64]{2,3,1,0:T(8,128)} %get-tuple-element.330, f32[40,64,64]{1,2,0:T(8,128)} %copy.119, f32[2,40,64]{2,1,0:T(8,128)S(1)} %copy-done.23, bf16[2,64,40,64]{3,2,1,0:T(8,128)(2,1)} %reshape.124), kind=kOutput, calls=%fused_computation.64 | convolution fusion | flops 252313600 | bytes 3952640 | tf_op jit(solution)/shard_map/nhkv,nthv->nthk/dot_general | solution.py:29
  352.5 4.1 multiply_reduce_fusion
  359.9 6.5 %fusion.9 = f32[2,64,40,64]{1,3,2,0:T(8,128)} fusion(f32[2,40,64,64]{3,2,1,0:T(8,128)S(1)} %fusion.21, f32[2,40,64,64]{3,2,1,0:T(8,128)S(1)} %copy-done.16, f32[2,40,64]{2,1,0:T(8,128)S(1)} %get-tuple-element.494, pred[64,64]{1,0:T(8,128)(4,1)S(1)} %iota_compare_fusion, f32[2,64,40,64]{1,3,2,0:T(8,128)S(1)} %copy-done.4, f32[2,64,40,64]{1,3,2,0:T(8,128)S(1)} %copy.89, ...), kind=kOutput, calls=%fused_computation.36 | convolution fusion | flops 254279680 | bytes 7888896 | tf_op jit(solution)/shard_map/nhts,nshk->nthk/dot_general | solution.py:29
  366.4 11.1 %multiply_subtract_fusion = (f32[2,64,40,64]{1,3,2,0:T(8,128)}, f32[2,64,40,64]{1,3,2,0:T(8,128)}, bf16[2,64,40,64]{1,3,2,0:T(8,128)(2,1)}, bf16[2,64,40,64]{1,3,2,0:T(8,128)(2,1)}, f32[2,64,40]{1,2,0:T(8,128)}) fusion(f32[2,64,40,64]{1,3,2,0:T(8,128)S(1)} %copy-done.4, f32[2,64,40,64]{1,3,2,0:T(8,128)S(1)} %copy-done.7, f32[2,64,40,64]{1,3,2,0:T(8,128)} %fusion.9, ...), kind=kOutput, calls=%fused_computation.39 | convolution fusion | flops 258862080 | bytes 13203456 | tf_op jit(solution)/shard_map/nhst,nshk->nthk/dot_general | solution.py:29
  380.7 3.5 fusion.83
  387.4 5.0 subtract_subtract_fusion
  403.0 6.6 %fusion.23 = f32[2,40,64,64]{2,3,1,0:T(8,128)} fusion(f32[2,40,64,64]{2,3,1,0:T(8,128)S(1)} %copy-done.13, f32[40,64,64]{1,2,0:T(8,128)S(1)} %copy-done.18, f32[2,40,64]{2,1,0:T(8,128)S(1)} %copy-done.24, f32[2,64,40,64]{1,3,2,0:T(8,128)S(1)} %copy-done.5, f32[2,64,40,64]{1,3,2,0:T(8,128)S(1)} %copy.89, f32[2,40,64]{2,1,0:T(8,128)S(1)} %copy-done.22), kind=kOutput, calls=%fused_computation.63 | convolution fusion | flops 252968960 | bytes 5939200 | tf_op jit(solution)/shard_map/nthk,nhkv->nthv/dot_general | solution.py:29
  411.1 7.4 %fusion.7 = bf16[2,64,40,64]{3,1,2,0:T(8,128)(2,1)} fusion(f32[2,40,64,64]{2,3,1,0:T(8,128)} %fusion.23, f32[2,40,64,64]{3,2,1,0:T(8,128)} %fusion.52, f32[2,64,40]{1,2,0:T(8,128)S(1)} %copy-done.26, pred[64,64]{1,0:T(8,128)(4,1)S(1)} %iota_compare_fusion, bf16[2,64,40,64]{3,2,1,0:T(8,128)(2,1)} %reshape.125), kind=kOutput, calls=%fused_computation.30 | convolution fusion | flops 253624320 | bytes 3956736 | tf_op jit(solution)/shard_map/nhst,nshv->nthv/dot_general | solution.py:29
  418.6 37.4 %all-reduce = (f32[2560]{0:T(1024)S(1)}, f32[2560]{0:T(1024)S(1)}) all-reduce(f32[2560]{0:T(1024)S(1)} %get-tuple-element.492, f32[2560]{0:T(1024)S(1)} %copy-done.29), channel_id=1, replica_groups=mesh['seq'=16,'dp'=2] {'seq','dp'}, use_global_device_ids=true, to_apply=%region_16.17 | all-reduce | flops 5120 | bytes 40960 | tf_op jit(solution)/shard_map/psum | solution.py:249
  463.3 8.7 %fusion.22 = f32[2,40,64,64]{2,3,1,0:T(8,128)S(1)} fusion(f32[2,40,64,64]{2,3,1,0:T(8,128)} %get-tuple-element.325, f32[40,64,64]{1,2,0:T(8,128)} %copy.103, f32[2,40,64]{2,1,0:T(8,128)S(1)} %get-tuple-element.321, f32[2,64,40,64]{1,3,2,0:T(8,128)} %copy.91, f32[2,64,40,64]{1,3,2,0:T(8,128)S(1)} %copy.89, f32[2,64,40,64]{1,3,2,0:T(8,128)} %copy.90), kind=kOutput, calls=%fused_computation.62 | convolution fusion | flops 252968960 | bytes 7229440 | tf_op jit(solution)/shard_map/nthk,nhkv->nthv/dot_general | solution.py:29
  485.3 59.9 %all-reduce.4.cloned.1.call-done = (f32[2560,128]{0,1:T(8,128)}, f32[2560,128]{1,0:T(8,128)}) async-done(((f32[2560,128]{0,1:T(8,128)}, f32[2560,128]{1,0:T(8,128)}), (f32[2560,128]{0,1:T(8,128)}, f32[2560,128]{1,0:T(8,128)})) %all-reduce.4.cloned.1.call-update) | async-done | bytes 2621456 | tf_op jit(solution)/shard_map/psum | solution.py:249
  (177 shorter events, 202.2 us)
Async XLA Ops:
  7.2 173.4 %all-gather.7.cloned.1.call-start = ((), (), s32[]{:S(2)}) async-start(), calls=%async_computation | async-start | bytes 22282240 | tf_op jit(solution)/shard_map/all_gather | solution.py:16
  18.9 9.7 %copy-start.21 = (f32[2,40,64]{2,1,0:T(8,128)}, f32[2,40,64]{2,1,0:T(8,128)S(1)}, u32[]{:S(2)}) copy-start(f32[2,40,64]{2,1,0:T(8,128)S(1)} %get-tuple-element.495) | copy-start | bytes 61444
  53.7 228.2 %all-gather.9.cloned.1.call-start = ((), (), s32[]{:S(2)}) async-start(), calls=%async_computation.1 | async-start | bytes 22282240 | tf_op jit(solution)/shard_map/all_gather | solution.py:16
  105.4 439.8 %all-reduce.4.cloned.1.call-start = ((), (), s32[]{:S(2)}) async-start(), calls=%async_computation.2 | async-start | bytes 5242880 | tf_op jit(solution)/shard_map/psum | solution.py:249
  166.0 6.9 %copy-start.6 = (f32[2,64,40,64]{1,3,2,0:T(8,128)S(1)}, f32[2,64,40,64]{1,3,2,0:T(8,128)}, u32[]{:S(2)}) copy-start(f32[2,64,40,64]{1,3,2,0:T(8,128)} %copy.91) | copy-start | bytes 3932164
  168.8 4.1 copy-start.1
  168.8 4.1 copy-start.3
  346.0 6.4 %copy-start.8 = (f32[2,40,64,64]{2,3,1,0:T(8,128)S(1)}, f32[2,40,64,64]{2,3,1,0:T(8,128)}, u32[]{:S(2)}) copy-start(f32[2,40,64,64]{2,3,1,0:T(8,128)} %get-tuple-element.773) | copy-start | bytes 3932164
  346.0 6.4 %copy-start.11 = (f32[2,40,64,64]{2,3,1,0:T(8,128)S(1)}, f32[2,40,64,64]{2,3,1,0:T(8,128)}, u32[]{:S(2)}) copy-start(f32[2,40,64,64]{2,3,1,0:T(8,128)} %get-tuple-element.325) | copy-start | bytes 3932164
  346.0 6.4 %copy-start.12 = (f32[2,40,64,64]{2,3,1,0:T(8,128)S(1)}, f32[2,40,64,64]{2,3,1,0:T(8,128)}, u32[]{:S(2)}) copy-start(f32[2,40,64,64]{2,3,1,0:T(8,128)} %get-tuple-element.330) | copy-start | bytes 3932164
  352.5 4.1 copy-start.10
  352.5 4.1 copy-start.17
  359.9 6.5 %copy-start.7 = (f32[2,64,40,64]{1,3,2,0:T(8,128)S(1)}, f32[2,64,40,64]{1,3,2,0:T(8,128)}, u32[]{:S(2)}) copy-start(f32[2,64,40,64]{1,3,2,0:T(8,128)} %copy.91) | copy-start | bytes 3932164
  359.9 6.5 %copy-start.22 = (f32[2,40,64]{2,1,0:T(8,128)S(1)}, f32[2,40,64]{2,1,0:T(8,128)}, u32[]{:S(2)}) copy-start(f32[2,40,64]{2,1,0:T(8,128)} %copy-done.21) | copy-start | bytes 61444
  359.9 6.5 %copy-start.25 = (f32[2,64,40]{1,2,0:T(8,128)S(1)}, f32[2,64,40]{1,2,0:T(8,128)}, u32[]{:S(2)}) copy-start(f32[2,64,40]{1,2,0:T(8,128)} %fusion.5) | copy-start | bytes 61444
  398.9 3.9 copy-start.5
  398.9 3.9 copy-start.13
  398.9 4.1 copy-start.18
  398.9 4.1 copy-start.24
  403.0 6.6 %copy-start.20 = (bf16[1,128,2560]{2,1,0:T(8,128)(2,1)S(1)}, bf16[1,128,2560]{2,1,0:T(8,128)(2,1)}, u32[]{:S(2)}) copy-start(bf16[1,128,2560]{2,1,0:T(8,128)(2,1)} %param.20) | copy-start | bytes 1966084
  411.1 7.5 %copy-start.29 = (f32[2560]{0:T(1024)S(1)}, f32[2560]{0:T(1024)}, u32[]{:S(2)}) copy-start(f32[2560]{0:T(1024)} %multiply_reduce_fusion.2) | copy-start | bytes 30724
  463.3 8.7 %copy-start.9 = (bf16[2,64,40,64]{3,2,1,0:T(8,128)(2,1)S(1)}, bf16[2,64,40,64]{3,2,1,0:T(8,128)(2,1)}, u32[]{:S(2)}) copy-start(bf16[2,64,40,64]{3,2,1,0:T(8,128)(2,1)} %reshape.124) | copy-start | bytes 1966084
  463.3 8.7 %copy-start.15 = (f32[2,40,64,64]{3,2,1,0:T(8,128)S(1)}, f32[2,40,64,64]{3,2,1,0:T(8,128)}, u32[]{:S(2)}) copy-start(f32[2,40,64,64]{3,2,1,0:T(8,128)} %fusion.52) | copy-start | bytes 3932164
  476.9 3.6 copy-start.19
  (9 other events, 22.0 us)
Sparse Core Ops, SparseCore 0:
  53.8 117.4 all-gather.6
  172.8 108.9 all-gather.8
  411.2 133.9 all-reduce.3
where the time goes:
time: 564 us; the launch traced here: 555 us
  waiting for transfers between devices  157 us (28%)
  local copies, waits for them, and re-layouts  125 us (22%)
  other arithmetic  87.2 us (15%)
  blocking collectives  87 us (15%)
  matrix products  84.5 us (15%)
  between operations  14.3 us (3%)
    all_gather x2, waiting for transfers between devices, carried_in(): gathered = jax.tree.map(lambda a: lax.all_gather(a, axis), part)  97 us
    dot_general x12, matrix products, contract(): jnp.einsum(pattern, left, right, precision=HIGH, preferred_element_type=j...  76 us
    psum x1, waiting for transfers between devices, per_device(): whole = lax.psum((sums[0], sums[1], sums[2], sums[3]), ('seq', 'dp'))  59.9 us
    all_gather x2, blocking collectives, carried_in(): gathered = jax.tree.map(lambda a: lax.all_gather(a, axis), part)  49.6 us
    add x15, other arithmetic, follow(): return (earlier[0] * later[0], later[0][..., None] * earlier[1] + later[1])  49.2 us
    psum x1, blocking collectives, per_device(): whole = lax.psum((sums[0], sums[1], sums[2], sums[3]), ('seq', 'dp'))  37.4 us
    dynamic_update_slice x8, local copies, waits for them, and re-layouts, compose(): return lax.scan(advance, initial, (decays, own_states), reverse=backward)  21.4 us
    convert_element_type x8, local copies, waits for them, and re-layouts, flatten(): return member.reshape(tokens, feature_span).astype(jnp.bfloat16)  14.5 us
  transfers between devices with their start and end apart: 3, of which 2 were waited for; matrix products, arithmetic and copies ran while one was open for 21% of the time, Pallas kernels for 0%

commit v1 on v0

--- a/solution.py
+++ b/solution.py
@@ -246,7 +246,7 @@
     sums = collected_outcomes[5]
     dp_count = lax.axis_size("dp")
     share_rows = fading_lowering_array.shape[0] // dp_count
-    whole = lax.psum((sums[0], sums[1], sums[2], sums[3]), ("seq", "dp"))
+    whole = lax.psum(lax.psum((sums[0], sums[1], sums[2], sums[3]), "dp"), "seq")
     offset = lax.axis_index("dp") * share_rows
     reduced = tuple((lax.dynamic_slice_in_dim(member, offset, share_rows, 0) for member in whole))
     return (

time: 564 us -> 599 us (1.062)
  blocking collectives: 87 us -> 117 us
  waiting for transfers between devices: 157 us -> 164 us
    psum x1 -> x2, blocking collectives: 37.4 us -> 67.6 us  [the longest x1 60.5 us: per_device(): lax.psum(lax.psum((sums[0], sums[1], sums[2], sums[3]), 'dp'), 'seq')]
    all_gather x2, waiting for transfers between devices: 97 us -> 116 us  [carried_in(): gathered = jax.tree.map(lambda a: lax.all_gather(a, axis), part)]
    psum x1 -> x2, waiting for transfers between devices: 59.9 us -> 47.4 us  [the longest x1 47.2 us: per_device(): lax.psum((sums[0], sums[1], sums[2], sums[3]), 'dp')]
  transfers between devices with their start and end apart: 3 -> 4, of which waited for: 2 -> 4; matrix products, arithmetic and copies ran while one was open for 21% -> 21% of each run, Pallas kernels for 0% -> 0%
where the time goes in v1:
time: 599 us; the launch traced here: 591 us
  waiting for transfers between devices  164 us (27%)
  local copies, waits for them, and re-layouts  124 us (21%)
  blocking collectives  117 us (20%)
  other arithmetic  86.2 us (14%)
  matrix products  84.8 us (14%)
  between operations  14.3 us (2%)
    all_gather x2, waiting for transfers between devices, carried_in(): gathered = jax.tree.map(lambda a: lax.all_gather(a, axis), part)  116 us
    dot_general x12, matrix products, contract(): jnp.einsum(pattern, left, right, precision=HIGH, preferred_element_type=j...  76.4 us
    psum x1, blocking collectives, per_device(): lax.psum(lax.psum((sums[0], sums[1], sums[2], sums[3]), 'dp'), 'seq')  60.5 us
    all_gather x2, blocking collectives, carried_in(): gathered = jax.tree.map(lambda a: lax.all_gather(a, axis), part)  49.7 us
    add x15, other arithmetic, follow(): return (earlier[0] * later[0], later[0][..., None] * earlier[1] + later[1])  49.2 us
    psum x1, waiting for transfers between devices, per_device(): lax.psum((sums[0], sums[1], sums[2], sums[3]), 'dp')  47.2 us
    dynamic_update_slice x8, local copies, waits for them, and re-layouts, compose(): return lax.scan(advance, initial, (decays, own_states), reverse=backward)  21.6 us
    convert_element_type x8, local copies, waits for them, and re-layouts, flatten(): return member.reshape(tokens, feature_span).astype(jnp.bfloat16)  14.6 us
  transfers between devices with their start and end apart: 4, of which 4 were waited for; matrix products, arithmetic and copies ran while one was open for 21% of the time, Pallas kernels for 0%

profile of v1, /device:TPU:0, one launch (start us, length us, event | category | flops | bytes accessed | tf_op | source)
XLA Modules:
  0.0 590.7 jit_solution(2860252752915887187)
XLA Ops:
  28.6 5.5 fusion.57
  35.9 17.7 %while.66 = (s32[]{:T(128)}, f32[40,64]{1,0:T(8,128)S(1)}, f32[40,64,64]{2,1,0:T(8,128)}, f32[2,40,64]{2,1,0:T(8,128)S(1)}, f32[2,40,64,64]{2,3,1,0:T(8,128)}, /...) while((s32[]{:T(128)}, f32[40,64]{1,0:T(8,128)S(1)}, ...), condition=%wide.region_3.4_spmd.clone, body=%wide.region_2.3_spmd.clone.sunk | while | flops 499203 | bytes 6646389 | solution.py:62
  44.6 3.6 select_bitcast_fusion.4
  62.6 3.6 copy.91
  66.2 7.0 %fusion.50 = f32[2,40,64,64]{2,3,1,0:T(8,128)} fusion(f32[2,64,40,64]{1,3,2,0:T(8,128)} %copy.91, bf16[2,64,40,64]{3,2,1,0:T(8,128)(2,1)} %reshape.125, f32[2,64,40,64]{1,3,2,0:T(8,128)S(1)} %copy.89, f32[2,64,40,64]{1,3,2,0:T(8,128)} %copy.90), kind=kOutput, calls=%fused_computation.85 | convolution fusion | flops 252313600 | bytes 5898240 | tf_op jit(solution)/shard_map/nchk,nchv->nhkv/dot_general | solution.py:29
  75.6 29.7 %while.67 = (s32[]{:T(128)}, f32[40,64]{1,0:T(8,128)S(1)}, f32[40,64,64]{2,1,0:T(8,128)}, f32[2,40,64]{2,1,0:T(8,128)}, f32[2,40,64,64]{2,3,1,0:T(8,128)}, /*ind...) while((s32[]{:T(128)}, f32[40,64]{1,0:T(8,128)S(1)}, ...), condition=%wide.region_8.9_spmd.clone, body=%wide.region_7.8_spmd.clone.sunk | while | flops 499204 | bytes 9257093 | solution.py:62
  96.3 3.6 select_bitcast_fusion.5
  106.2 27.8 %all-gather = f32[640,64]{1,0:T(8,128)} all-gather(f32[40,64]{1,0:T(8,128)S(1)} %get-tuple-element.322), channel_id=2, replica_groups=mesh['seq'=16,'dp'=2] {'seq'}, dimensions={0}, use_global_device_ids=true | all-gather | bytes 174080 | tf_op jit(solution)/shard_map/all_gather | solution.py:16
  134.0 21.9 %all-gather.2 = f32[640,64]{1,0:T(8,128)} all-gather(f32[40,64]{1,0:T(8,128)S(1)} %get-tuple-element.327), channel_id=4, replica_groups=mesh['seq'=16,'dp'=2] {'seq'}, dimensions={0}, use_global_device_ids=true | all-gather | bytes 174080 | tf_op jit(solution)/shard_map/all_gather | solution.py:16
  161.5 9.7 %all-gather.7.cloned.1.call-done = f32[640,64,64]{2,1,0:T(8,128)} async-done(((f32[40,64,64]{2,1,0:T(8,128)}), f32[640,64,64]{2,1,0:T(8,128)}) %all-gather.7.cloned.1.call-update) | async-done | bytes 10485776 | tf_op jit(solution)/shard_map/all_gather | solution.py:16
  175.2 106.6 %all-gather.9.cloned.1.call-done = f32[640,64,64]{2,1,0:T(8,128)} async-done(((f32[40,64,64]{2,1,0:T(8,128)}), f32[640,64,64]{2,1,0:T(8,128)}) %all-gather.9.cloned.1.call-update) | async-done | bytes 10485776 | tf_op jit(solution)/shard_map/all_gather | solution.py:16
  283.0 60.3 %while.65 = (s32[]{:T(128)}, f32[40,64,64]{2,1,0:T(8,128)}, s32[]{:T(128)}, f32[16,40,64]{2,1,0:T(8,128)}, f32[16,40,64,64]{3,2,1,0:T(8,128)}, /*index=5*/s32[]{:T(128)}, s32[]{:T(128)}, s32[]{:T(128)}, s32[]{:T(128)}) while((s32[]{:T(128)}, f32[40,64,64]{2,1,0:T(8,128)}, s32[]{:T(128)}, f32[16,40,64]{2,1,0:T(8,128)}, ...), condition=%wide.region_10.11_spmd, body=%wide.region_9.10_spmd.sunk | while | flops 327686 | bytes 1996947 | solution.py:25
  346.2 6.4 %fusion.24 = f32[2,40,64,64]{3,2,1,0:T(8,128)} fusion(f32[2,40,64,64]{2,3,1,0:T(8,128)} %get-tuple-element.330, f32[40,64,64]{1,2,0:T(8,128)} %copy.119, f32[2,40,64]{2,1,0:T(8,128)S(1)} %copy-done.23, bf16[2,64,40,64]{3,2,1,0:T(8,128)(2,1)} %reshape.124), kind=kOutput, calls=%fused_computation.64 | convolution fusion | flops 252313600 | bytes 3952640 | tf_op jit(solution)/shard_map/nhkv,nthv->nthk/dot_general | solution.py:29
  352.7 4.1 multiply_reduce_fusion
  360.1 6.7 %fusion.9 = f32[2,64,40,64]{1,3,2,0:T(8,128)} fusion(f32[2,40,64,64]{3,2,1,0:T(8,128)S(1)} %fusion.21, f32[2,40,64,64]{3,2,1,0:T(8,128)S(1)} %copy-done.16, f32[2,40,64]{2,1,0:T(8,128)S(1)} %get-tuple-element.498, pred[64,64]{1,0:T(8,128)(4,1)S(1)} %iota_compare_fusion, f32[2,64,40,64]{1,3,2,0:T(8,128)S(1)} %copy-done.3, f32[2,64,40,64]{1,3,2,0:T(8,128)S(1)} %copy.89, ...), kind=kOutput, calls=%fused_computation.36 | convolution fusion | flops 254279680 | bytes 7888896 | tf_op jit(solution)/shard_map/nhts,nshk->nthk/dot_general | solution.py:29
  366.8 11.1 %multiply_subtract_fusion = (f32[2,64,40,64]{1,3,2,0:T(8,128)}, f32[2,64,40,64]{1,3,2,0:T(8,128)}, bf16[2,64,40,64]{1,3,2,0:T(8,128)(2,1)}, bf16[2,64,40,64]{1,3,2,0:T(8,128)(2,1)}, f32[2,64,40]{1,2,0:T(8,128)}) fusion(f32[2,64,40,64]{1,3,2,0:T(8,128)S(1)} %copy-done.3, f32[2,64,40,64]{1,3,2,0:T(8,128)S(1)} %copy-done.5, f32[2,64,40,64]{1,3,2,0:T(8,128)} %fusion.9, ...), kind=kOutput, calls=%fused_computation.39 | convolution fusion | flops 258862080 | bytes 13203456 | tf_op jit(solution)/shard_map/nhst,nshk->nthk/dot_general | solution.py:29
  387.8 4.9 subtract_subtract_fusion
  412.6 9.8 %fusion.52 = f32[2,40,64,64]{3,2,1,0:T(8,128)} fusion(f32[2,64,40,64]{1,3,2,0:T(8,128)} %copy.93, f32[2,64,40,64]{1,3,2,0:T(8,128)S(1)} %copy.89, f32[2,40,64]{2,1,0:T(8,128)S(1)} %get-tuple-element.498, f32[2,64,40,64]{1,3,2,0:T(8,128)} %copy.91, f32[2,64,40,64]{1,3,2,0:T(8,128)S(1)} %copy-done.2), kind=kOutput, calls=%fused_computation.86 | convolution fusion | flops 253296640 | bytes 6574080 | tf_op jit(solution)/shard_map/nthk,nshk->nhts/dot_general | solution.py:29
  422.5 6.7 %fusion.23 = f32[2,40,64,64]{2,3,1,0:T(8,128)} fusion(f32[2,40,64,64]{2,3,1,0:T(8,128)S(1)} %copy-done.13, f32[40,64,64]{1,2,0:T(8,128)S(1)} %copy-done.18, f32[2,40,64]{2,1,0:T(8,128)S(1)} %copy-done.24, f32[2,64,40,64]{1,3,2,0:T(8,128)S(1)} %copy-done.4, f32[2,64,40,64]{1,3,2,0:T(8,128)S(1)} %copy.89, f32[2,40,64]{2,1,0:T(8,128)S(1)} %copy-done.22), kind=kOutput, calls=%fused_computation.63 | convolution fusion | flops 252968960 | bytes 5939200 | tf_op jit(solution)/shard_map/nthk,nhkv->nthv/dot_general | solution.py:29
  429.2 47.2 %all-reduce.9.cloned.1.call-done = (f32[2560,128]{0,1:T(8,128)}, f32[2560,128]{1,0:T(8,128)}) async-done(((f32[2560,128]{0,1:T(8,128)}, f32[2560,128]{1,0:T(8,128)}), (f32[2560,128]{0,1:T(8,128)}, f32[2560,128]{1,0:T(8,128)})) %all-reduce.9.cloned.1.call-update) | async-done | bytes 2621456 | tf_op jit(solution)/shard_map/psum | solution.py:249
  476.4 7.1 %fusion.7 = bf16[2,64,40,64]{3,1,2,0:T(8,128)(2,1)} fusion(f32[2,40,64,64]{2,3,1,0:T(8,128)} %fusion.23, f32[2,40,64,64]{3,2,1,0:T(8,128)} %fusion.52, f32[2,64,40]{1,2,0:T(8,128)S(1)} %copy-done.26, pred[64,64]{1,0:T(8,128)(4,1)S(1)} %iota_compare_fusion, bf16[2,64,40,64]{3,2,1,0:T(8,128)(2,1)} %reshape.125), kind=kOutput, calls=%fused_computation.30 | convolution fusion | flops 253624320 | bytes 3956736 | tf_op jit(solution)/shard_map/nhst,nshv->nthv/dot_general | solution.py:29
  483.5 7.1 %all-reduce.2 = (f32[2560]{0:T(1024)S(1)}, f32[2560]{0:T(1024)S(1)}) all-reduce(f32[2560]{0:T(1024)S(1)} %get-tuple-element.496, f32[2560]{0:T(1024)S(1)} %multiply_reduce_fusion.2), channel_id=1, replica_groups=mesh['seq'=16,'dp'=2] {'dp'}, use_global_device_ids=true, to_apply=%region_18.19 | all-reduce | flops 5120 | bytes 40960 | tf_op jit(solution)/shard_map/psum | solution.py:249
  490.6 60.5 %all-reduce = (f32[2560]{0:T(1024)S(1)}, f32[2560]{0:T(1024)S(1)}) all-reduce(f32[2560]{0:T(1024)S(1)} %get-tuple-element.479, f32[2560]{0:T(1024)S(1)} %get-tuple-element.480), channel_id=1, replica_groups=mesh['seq'=16,'dp'=2] {'seq'}, use_global_device_ids=true, to_apply=%region_19.20 | all-reduce | flops 5120 | bytes 40960 | tf_op jit(solution)/shard_map/psum | solution.py:249
  558.6 8.8 %fusion.22 = f32[2,40,64,64]{2,3,1,0:T(8,128)S(1)} fusion(f32[2,40,64,64]{2,3,1,0:T(8,128)} %get-tuple-element.325, f32[40,64,64]{1,2,0:T(8,128)} %copy.103, f32[2,40,64]{2,1,0:T(8,128)S(1)} %get-tuple-element.321, f32[2,64,40,64]{1,3,2,0:T(8,128)} %copy.91, f32[2,64,40,64]{1,3,2,0:T(8,128)S(1)} %copy.89, f32[2,64,40,64]{1,3,2,0:T(8,128)} %copy.90), kind=kOutput, calls=%fused_computation.62 | convolution fusion | flops 252968960 | bytes 7229440 | tf_op jit(solution)/shard_map/nthk,nhkv->nthv/dot_general | solution.py:29
  (181 shorter events, 206.4 us)
Async XLA Ops:
  7.2 164.0 %all-gather.7.cloned.1.call-start = ((), (), s32[]{:S(2)}) async-start(), calls=%async_computation | async-start | bytes 22282240 | tf_op jit(solution)/shard_map/all_gather | solution.py:16
  18.9 9.6 %copy-start.21 = (f32[2,40,64]{2,1,0:T(8,128)}, f32[2,40,64]{2,1,0:T(8,128)S(1)}, u32[]{:S(2)}) copy-start(f32[2,40,64]{2,1,0:T(8,128)S(1)} %get-tuple-element.499) | copy-start | bytes 61444
  53.6 228.2 %all-gather.9.cloned.1.call-start = ((), (), s32[]{:S(2)}) async-start(), calls=%async_computation.1 | async-start | bytes 22282240 | tf_op jit(solution)/shard_map/all_gather | solution.py:16
  105.3 371.0 %all-reduce.9.cloned.1.call-start = ((), (), s32[]{:S(2)}) async-start(), calls=%async_computation.3 | async-start | bytes 5242880 | tf_op jit(solution)/shard_map/psum | solution.py:249
  106.2 53.0 %copy-start.7 = (bf16[2,64,40,64]{3,2,1,0:T(8,128)(2,1)S(1)}, bf16[2,64,40,64]{3,2,1,0:T(8,128)(2,1)}, u32[]{:S(2)}) copy-start(bf16[2,64,40,64]{3,2,1,0:T(8,128)(2,1)} %reshape.124) | copy-start | bytes 1966084
  106.2 53.0 %copy-start.9 = (bf16[2,64,40,64]{3,2,1,0:T(8,128)(2,1)S(1)}, bf16[2,64,40,64]{3,2,1,0:T(8,128)(2,1)}, u32[]{:S(2)}) copy-start(bf16[2,64,40,64]{3,2,1,0:T(8,128)(2,1)} %reshape.125) | copy-start | bytes 1966084
  346.2 6.4 %copy-start.6 = (f32[2,40,64,64]{2,3,1,0:T(8,128)S(1)}, f32[2,40,64,64]{2,3,1,0:T(8,128)}, u32[]{:S(2)}) copy-start(f32[2,40,64,64]{2,3,1,0:T(8,128)} %get-tuple-element.781) | copy-start | bytes 3932164
  346.2 6.4 %copy-start.11 = (f32[2,40,64,64]{2,3,1,0:T(8,128)S(1)}, f32[2,40,64,64]{2,3,1,0:T(8,128)}, u32[]{:S(2)}) copy-start(f32[2,40,64,64]{2,3,1,0:T(8,128)} %get-tuple-element.325) | copy-start | bytes 3932164
  346.2 6.4 %copy-start.12 = (f32[2,40,64,64]{2,3,1,0:T(8,128)S(1)}, f32[2,40,64,64]{2,3,1,0:T(8,128)}, u32[]{:S(2)}) copy-start(f32[2,40,64,64]{2,3,1,0:T(8,128)} %get-tuple-element.330) | copy-start | bytes 3932164
  352.7 4.1 copy-start.10
  352.7 4.1 copy-start.17
  360.1 6.7 %copy-start.5 = (f32[2,64,40,64]{1,3,2,0:T(8,128)S(1)}, f32[2,64,40,64]{1,3,2,0:T(8,128)}, u32[]{:S(2)}) copy-start(f32[2,64,40,64]{1,3,2,0:T(8,128)} %copy.91) | copy-start | bytes 3932164
  360.1 6.7 %copy-start.22 = (f32[2,40,64]{2,1,0:T(8,128)S(1)}, f32[2,40,64]{2,1,0:T(8,128)}, u32[]{:S(2)}) copy-start(f32[2,40,64]{2,1,0:T(8,128)} %copy-done.21) | copy-start | bytes 61444
  360.1 6.7 %copy-start.25 = (f32[2,64,40]{1,2,0:T(8,128)S(1)}, f32[2,64,40]{1,2,0:T(8,128)}, u32[]{:S(2)}) copy-start(f32[2,64,40]{1,2,0:T(8,128)} %fusion.5) | copy-start | bytes 61444
  398.8 4.3 copy-start.20
  404.6 176.2 %all-reduce.7.cloned.1.call-start = ((), (), s32[]{:S(2)}) async-start(), calls=%async_computation.2 | async-start | bytes 5242880 | tf_op jit(solution)/shard_map/psum | solution.py:249
  412.6 9.8 %copy-start.4 = (f32[2,64,40,64]{1,3,2,0:T(8,128)S(1)}, f32[2,64,40,64]{1,3,2,0:T(8,128)}, u32[]{:S(2)}) copy-start(f32[2,64,40,64]{1,3,2,0:T(8,128)} %copy.93) | copy-start | bytes 3932164
  412.6 9.8 %copy-start.13 = (f32[2,40,64,64]{2,3,1,0:T(8,128)S(1)}, f32[2,40,64,64]{2,3,1,0:T(8,128)}, u32[]{:S(2)}) copy-start(f32[2,40,64,64]{2,3,1,0:T(8,128)} %get-tuple-element.330) | copy-start | bytes 3932164
  412.6 9.9 %copy-start.18 = (f32[40,64,64]{1,2,0:T(8,128)S(1)}, f32[40,64,64]{1,2,0:T(8,128)}, u32[]{:S(2)}) copy-start(f32[40,64,64]{1,2,0:T(8,128)} %copy.119) | copy-start | bytes 1966084
  412.6 9.9 %copy-start.24 = (f32[2,40,64]{2,1,0:T(8,128)S(1)}, f32[2,40,64]{2,1,0:T(8,128)}, u32[]{:S(2)}) copy-start(f32[2,40,64]{2,1,0:T(8,128)} %get-tuple-element.326) | copy-start | bytes 61444
  429.2 47.2 %copy-start.26 = (f32[2,64,40]{1,2,0:T(8,128)S(1)}, f32[2,64,40]{1,2,0:T(8,128)}, u32[]{:S(2)}) copy-start(f32[2,64,40]{1,2,0:T(8,128)} %get-tuple-element.495) | copy-start | bytes 61444
  558.6 8.8 %copy-start.8 = (bf16[2,64,40,64]{3,2,1,0:T(8,128)(2,1)S(1)}, bf16[2,64,40,64]{3,2,1,0:T(8,128)(2,1)}, u32[]{:S(2)}) copy-start(bf16[2,64,40,64]{3,2,1,0:T(8,128)(2,1)} %reshape.124) | copy-start | bytes 1966084
  558.6 8.8 %copy-start.15 = (f32[2,40,64,64]{3,2,1,0:T(8,128)S(1)}, f32[2,40,64,64]{3,2,1,0:T(8,128)}, u32[]{:S(2)}) copy-start(f32[2,40,64,64]{3,2,1,0:T(8,128)} %fusion.52) | copy-start | bytes 3932164
  572.3 3.6 copy-start.19
  (10 other events, 23.0 us)
Sparse Core Ops, SparseCore 0:
  53.7 117.4 all-gather.6
  172.8 108.9 all-gather.8
  404.7 71.6 all-reduce.8
  479.9 100.8 all-reduce.6
